TPU v7x, 32 devices: a whole 2x2x4 slice. The times are simulated.
32 devices in a mesh: row: 4 (over y, core), col: 8 (over z, x).
Axes of the slice: x: 2, y: 2, z: 4, core: 2. Of those that a mesh axis runs over, the one named last changes fastest.
Arguments:
- matrix: float32 [16384, 16384], P('row', 'col'), as said below
Outputs:
- hess_panel: float32 [16384, 8], P('row')
- reflectors: float32 [16384, 8], P('row')
- wy_products: float32 [16384, 8], P('row')
- wy_factor: float32 [8, 8], replicated
Inputs may be any that keep to these rules, and one draw needn't show every extreme that they name: Entries matrix[i+1, i] lie within 2.5 +- 6 / sqrt(16384); every other entry within +- 6 / sqrt(16384).
All inputs are finite; a program needn't handle non-finite values.
Results may differ from a plain program's by a relative error of at most 0.0003.
Values sent between devices are 32-bit elements; how exact they have to be, the bound alone decides.
A program may use at most 128 MiB of HBM per device.

v0:
```python
import jax
import jax.numpy as jnp
from jax import lax
from jax.sharding import PartitionSpec as P

NB = 8


def spread(value, axis, root):
    mine = lax.axis_index(axis) == root
    return lax.psum(jnp.where(mine, value, jnp.zeros_like(value)), axis)


def shards(matrix):
    exact = lax.Precision.HIGHEST
    rows_local, cols_local = matrix.shape
    row_ids = lax.axis_index("row") * rows_local + lax.iota(jnp.int32, rows_local)
    panel = spread(matrix[:, :NB], "col", 0)
    top_ids = lax.iota(jnp.int32, NB + 1)
    picker = (row_ids[None, :] == top_ids[:, None]).astype(jnp.float32)
    refl = jnp.zeros((rows_local, NB), jnp.float32)
    wy_prod = jnp.zeros((rows_local, NB), jnp.float32)
    factor = jnp.zeros((NB, NB), jnp.float32)
    refl_top = jnp.zeros((NB + 1, NB), jnp.float32)
    gram = jnp.zeros((NB, NB), jnp.float32)
    columns = []
    for column in range(NB):
        current = panel[:, column] - jnp.dot(wy_prod, refl_top[column], precision=exact)
        if column > 0:
            inner = lax.psum(jnp.dot(current, refl, precision=exact), "row")
            current = current - jnp.dot(
                refl, jnp.dot(inner, factor, precision=exact), precision=exact
            )
        below = jnp.where(row_ids > column, current, jnp.float32(0.0))
        sumsq, leading = lax.psum(
            (
                jnp.sum(below * below),
                jnp.sum(jnp.where(row_ids == column + 1, current, jnp.float32(0.0))),
            ),
            "row",
        )
        masked = jnp.where(row_ids > column, current, jnp.float32(0.0))
        length = jnp.sqrt(sumsq)
        orient = jnp.where(leading >= 0, jnp.float32(1.0), jnp.float32(-1.0))
        pivot_value = -orient * length
        vector = masked + jnp.where(row_ids == column + 1, orient * length, jnp.float32(0.0))
        vector = vector / jnp.sqrt(length * (length + jnp.abs(leading)))
        start = lax.axis_index("col") * cols_local
        received = spread(vector, "row", start // rows_local)
        piece = lax.dynamic_slice_in_dim(received, start % rows_local, cols_local, 0)
        coupling, vec_top = lax.psum(
            (jnp.dot(vector, refl, precision=exact), jnp.dot(picker, vector, precision=exact)),
            "row",
        )
        image = lax.psum(jnp.dot(matrix, piece, precision=exact), "col")
        new_y = image - jnp.dot(wy_prod, coupling, precision=exact)
        new_t = -jnp.dot(factor, coupling, precision=exact)
        factor = factor.at[:, column].set(new_t).at[column, column].set(jnp.float32(1.0))
        gram = (
            gram.at[:, column]
            .set(coupling)
            .at[column, :]
            .set(coupling)
            .at[column, column]
            .set(jnp.float32(2.0))
        )
        wy_prod = wy_prod.at[:, column].set(new_y)
        refl = refl.at[:, column].set(vector)
        refl_top = refl_top.at[:, column].set(vec_top)
        columns.append(
            jnp.where(
                row_ids <= column,
                current,
                jnp.where(row_ids == column + 1, pivot_value, jnp.float32(0.0)),
            )
        )
    return (jnp.stack(columns, axis=1), refl, wy_prod, factor)


def solution(mesh):
    return jax.shard_map(
        shards,
        mesh=mesh,
        in_specs=(P("row", "col"),),
        out_specs=(P("row", None), P("row", None), P("row", None), P()),
        check_vma=False,
    )
```

profile of v0, /device:TPU:0, one launch (start us, length us, event | category | flops | bytes accessed | tf_op | source)
XLA Modules:
  0.0 897.8 jit_solution(13445658246605330233)
XLA Ops:
  15.5 101.1 %all-reduce.22.cloned.1.call-done = f32[4096,8]{1,0:T(8,128)} async-done(((f32[4096,8]{1,0:T(8,128)}), f32[4096,8]{1,0:T(8,128)}) %all-reduce.22.cloned.1.call-update) | async-done | bytes 131088 | tf_op jit(solution)/shard_map/psum | solution.py:11
  116.7 15.4 %slice_reduce_fusion = (f32[4096]{0:T(1024)S(1)}, f32[4096]{0:T(1024)S(1)}, f32[4096]{0:T(1024)S(1)}, f32[4096]{0:T(1024)S(1)}, f32[4096]{0:T(1024)S(1)}, /*inde...) fusion(f32[4096,8]{1,0:T(8,128)} %all-reduce.22.cloned.1.call-done), kind=kLoop, calls=%fused_computation | loop fusion | bytes 262144 | tf_op jit(solution)/shard_map/slice | solution.py:28
  143.5 10.6 %all-reduce.18 = (f32[4096]{0:T(1024)S(1)}, f32[8]{0:T(128)S(1)}, f32[9]{0:T(128)S(1)}) all-reduce(f32[4096]{0:T(1024)S(1)} %broadcast_select_fusion.19, f32[8]{0:T(128)S(1)} %convolution_bitcast_fusion.36, f32[9]{0:T(128)S(1)} %convolution_bitcast_fusion.35), channel_id=1, replica_groups=mesh['row'=4,'col'=8] {'row'}, use_global_device_ids=true, to_apply=%region_6.7 | all-reduce | flops 4113 | bytes 32904 | tf_op jit(solution)/shard_map/psum | solution.py:11
  154.1 30.7 %fusion.122 = f32[1,4096]{1,0:T(1,128)S(1)} fusion(f32[2048,1]{0,1:T(1,128)S(1)} %bitcast.507, f32[4096,2048]{1,0:T(8,128)} %param.79), kind=kOutput, calls=%fused_computation.248 | convolution fusion | flops 100663296 | bytes 33579008 | tf_op jit(solution)/shard_map/dot_general | solution.py:55
  184.7 35.8 %psum.389 = f32[4096]{0:T(1024)S(1)} all-reduce(f32[4096]{0:T(1024)S(1)} %bitcast.450), channel_id=1, replica_groups=mesh['row'=4,'col'=8] {'col'}, use_global_device_ids=true, to_apply=%region_7.8 | all-reduce | flops 4096 | bytes 32768 | tf_op jit(solution)/shard_map/psum | solution.py:55
  241.9 10.3 %all-reduce.16 = (f32[4096]{0:T(1024)S(1)}, f32[8]{0:T(128)S(1)}, f32[9]{0:T(128)S(1)}) all-reduce(f32[4096]{0:T(1024)S(1)} %broadcast_select_fusion.17, f32[8]{0:T(128)S(1)} %convolution_bitcast_fusion.33, f32[9]{0:T(128)S(1)} %convolution_bitcast_fusion.32), channel_id=1, replica_groups=mesh['row'=4,'col'=8] {'row'}, use_global_device_ids=true, to_apply=%region_16.17 | all-reduce | flops 4113 | bytes 32904 | tf_op jit(solution)/shard_map/psum | solution.py:11
  253.3 30.7 %fusion.123 = f32[1,4096]{1,0:T(1,128)S(1)} fusion(f32[2048,1]{0,1:T(1,128)S(1)} %bitcast.508, f32[4096,2048]{1,0:T(8,128)} %param.79), kind=kOutput, calls=%fused_computation.249 | convolution fusion | flops 100663296 | bytes 33579008 | tf_op jit(solution)/shard_map/dot_general | solution.py:55
  284.0 33.0 %psum.396 = f32[4096]{0:T(1024)S(1)} all-reduce(f32[4096]{0:T(1024)S(1)} %bitcast.451), channel_id=1, replica_groups=mesh['row'=4,'col'=8] {'col'}, use_global_device_ids=true, to_apply=%region_17.18 | all-reduce | flops 4096 | bytes 32768 | tf_op jit(solution)/shard_map/psum | solution.py:55
  337.3 10.6 %all-reduce.14 = (f32[4096]{0:T(1024)S(1)}, f32[8]{0:T(128)S(1)}, f32[9,1]{0,1:T(1,128)S(1)}) all-reduce(f32[4096]{0:T(1024)S(1)} %get-tuple-element.558, f32[8]{0:T(128)S(1)} %convolution_bitcast_fusion.30, f32[9,1]{0,1:T(1,128)S(1)} %convolution_bitcast_fusion.29), channel_id=1, replica_groups=mesh['row'=4,'col'=8] {'row'}, use_global_device_ids=true, to_apply=%region_26.27 | all-reduce | flops 4113 | bytes 32904 | tf_op jit(solution)/shard_map/psum | solution.py:11
  350.0 30.7 %fusion.125 = f32[1,4096]{1,0:T(1,128)S(1)} fusion(f32[2048,1]{0,1:T(1,128)S(1)} %bitcast.509, f32[4096,2048]{1,0:T(8,128)} %param.79), kind=kOutput, calls=%fused_computation.251 | convolution fusion | flops 100663296 | bytes 33579008 | tf_op jit(solution)/shard_map/dot_general | solution.py:55
  380.7 33.0 %psum.403 = f32[4096]{0:T(1024)S(1)} all-reduce(f32[4096]{0:T(1024)S(1)} %bitcast.452), channel_id=1, replica_groups=mesh['row'=4,'col'=8] {'col'}, use_global_device_ids=true, to_apply=%region_27.28 | all-reduce | flops 4096 | bytes 32768 | tf_op jit(solution)/shard_map/psum | solution.py:55
  444.8 30.7 %fusion.127 = f32[1,4096]{1,0:T(1,128)S(1)} fusion(f32[2048,1]{0,1:T(1,128)S(1)} %bitcast.510, f32[4096,2048]{1,0:T(8,128)} %param.79), kind=kOutput, calls=%fused_computation.253 | convolution fusion | flops 100663296 | bytes 33579008 | tf_op jit(solution)/shard_map/dot_general | solution.py:55
  475.5 33.0 %psum.410 = f32[4096]{0:T(1024)S(1)} all-reduce(f32[4096]{0:T(1024)S(1)} %bitcast.453), channel_id=1, replica_groups=mesh['row'=4,'col'=8] {'col'}, use_global_device_ids=true, to_apply=%region_37.38 | all-reduce | flops 4096 | bytes 32768 | tf_op jit(solution)/shard_map/psum | solution.py:55
  528.5 10.6 %all-reduce.10 = (f32[4096]{0:T(1024)S(1)}, f32[8]{0:T(128)S(1)}, f32[9,1]{0,1:T(1,128)S(1)}) all-reduce(f32[4096]{0:T(1024)S(1)} %get-tuple-element.552, f32[8]{0:T(128)S(1)} %convolution_bitcast_fusion.24, f32[9,1]{0,1:T(1,128)S(1)} %convolution_bitcast_fusion.23), channel_id=1, replica_groups=mesh['row'=4,'col'=8] {'row'}, use_global_device_ids=true, to_apply=%region_46.47 | all-reduce | flops 4113 | bytes 32904 | tf_op jit(solution)/shard_map/psum | solution.py:11
  541.0 30.7 %fusion.129 = f32[1,4096]{1,0:T(1,128)S(1)} fusion(f32[2048,1]{0,1:T(1,128)S(1)} %bitcast.511, f32[4096,2048]{1,0:T(8,128)} %param.79), kind=kOutput, calls=%fused_computation.255 | convolution fusion | flops 100663296 | bytes 33579008 | tf_op jit(solution)/shard_map/dot_general | solution.py:55
  571.7 33.0 %psum.417 = f32[4096]{0:T(1024)S(1)} all-reduce(f32[4096]{0:T(1024)S(1)} %bitcast.454), channel_id=1, replica_groups=mesh['row'=4,'col'=8] {'col'}, use_global_device_ids=true, to_apply=%region_47.48 | all-reduce | flops 4096 | bytes 32768 | tf_op jit(solution)/shard_map/psum | solution.py:55
  635.9 30.7 %fusion.131 = f32[1,4096]{1,0:T(1,128)S(1)} fusion(f32[2048,1]{0,1:T(1,128)S(1)} %bitcast.512, f32[4096,2048]{1,0:T(8,128)} %param.79), kind=kOutput, calls=%fused_computation.257 | convolution fusion | flops 100663296 | bytes 33579008 | tf_op jit(solution)/shard_map/dot_general | solution.py:55
  666.6 33.0 %psum.424 = f32[4096]{0:T(1024)S(1)} all-reduce(f32[4096]{0:T(1024)S(1)} %bitcast.455), channel_id=1, replica_groups=mesh['row'=4,'col'=8] {'col'}, use_global_device_ids=true, to_apply=%region_57.58 | all-reduce | flops 4096 | bytes 32768 | tf_op jit(solution)/shard_map/psum | solution.py:55
  719.4 10.6 %all-reduce.6 = (f32[4096]{0:T(1024)S(1)}, f32[8]{0:T(128)S(1)}, f32[9,1]{0,1:T(1,128)S(1)}) all-reduce(f32[4096]{0:T(1024)S(1)} %get-tuple-element.546, f32[8]{0:T(128)S(1)} %convolution_bitcast_fusion.18, f32[9,1]{0,1:T(1,128)S(1)} %convolution_bitcast_fusion.17), channel_id=1, replica_groups=mesh['row'=4,'col'=8] {'row'}, use_global_device_ids=true, to_apply=%region_66.67 | all-reduce | flops 4113 | bytes 32904 | tf_op jit(solution)/shard_map/psum | solution.py:11
  732.0 30.7 %fusion.133 = f32[1,4096]{1,0:T(1,128)S(1)} fusion(f32[2048,1]{0,1:T(1,128)S(1)} %bitcast.513, f32[4096,2048]{1,0:T(8,128)} %param.79), kind=kOutput, calls=%fused_computation.259 | convolution fusion | flops 100663296 | bytes 33579008 | tf_op jit(solution)/shard_map/dot_general | solution.py:55
  762.7 33.0 %psum.431 = f32[4096]{0:T(1024)S(1)} all-reduce(f32[4096]{0:T(1024)S(1)} %bitcast.456), channel_id=1, replica_groups=mesh['row'=4,'col'=8] {'col'}, use_global_device_ids=true, to_apply=%region_67.68 | all-reduce | flops 4096 | bytes 32768 | tf_op jit(solution)/shard_map/psum | solution.py:55
  813.8 10.3 %all-reduce.4 = (f32[4096]{0:T(1024)S(1)}, f32[8]{0:T(128)S(1)}) all-reduce(f32[4096]{0:T(1024)S(1)} %get-tuple-element.543, f32[8]{0:T(128)S(1)} %convolution_bitcast_fusion.15), channel_id=1, replica_groups=mesh['row'=4,'col'=8] {'row'}, use_global_device_ids=true, to_apply=%region_75.76 | all-reduce | flops 4104 | bytes 32832 | tf_op jit(solution)/shard_map/psum | solution.py:11
  825.9 30.7 %fusion.135 = f32[1,4096]{1,0:T(1,128)S(1)} fusion(f32[2048,1]{0,1:T(1,128)S(1)} %bitcast.506, f32[4096,2048]{1,0:T(8,128)} %param.79), kind=kOutput, calls=%fused_computation.261 | convolution fusion | flops 100663296 | bytes 33579008 | tf_op jit(solution)/shard_map/dot_general | solution.py:55
  856.6 33.0 %psum.438 = f32[4096]{0:T(1024)S(1)} all-reduce(f32[4096]{0:T(1024)S(1)} %bitcast.457), channel_id=1, replica_groups=mesh['row'=4,'col'=8] {'col'}, use_global_device_ids=true, to_apply=%region_76.77 | all-reduce | flops 4096 | bytes 32768 | tf_op jit(solution)/shard_map/psum | solution.py:55
  (200 shorter events, 174.7 us)
Async XLA Ops:
  7.2 109.5 %all-reduce.22.cloned.1.call-start = ((), (), s32[]{:S(2)}) async-start(), calls=%async_computation | async-start | bytes 4194304 | tf_op jit(solution)/shard_map/psum | solution.py:11
  824.9 65.9 %copy-start = (f32[4096,8]{0,1:T(8,128)}, f32[4096,8]{0,1:T(8,128)S(1)}, u32[]{:S(2)}) copy-start(f32[4096,8]{0,1:T(8,128)S(1)} %scatter.189) | copy-start | bytes 393220
  890.0 0.9 copy-start.1
Sparse Core Ops, SparseCore 0:
  11.6 105.0 all-reduce.21
where the time goes:
time: 907 us; the launch traced here: 898 us
  blocking collectives  444 us (49%)
  matrix products  265 us (29%)
  waiting for transfers between devices  101 us (11%)
  between operations  31.3 us (3%)
  local copies, waits for them, and re-layouts  28.4 us (3%)
  other arithmetic  27.4 us (3%)
    psum x8, blocking collectives, shards(): image = lax.psum(jnp.dot(matrix, piece, precision=exact), 'col')  267 us
    dot_general x8, matrix products, shards(): image = lax.psum(jnp.dot(matrix, piece, precision=exact), 'col')  246 us
    psum x1, waiting for transfers between devices, spread(): return lax.psum(jnp.where(mine, value, jnp.zeros_like(value)), axis)  101 us
    psum x8, blocking collectives, spread(): return lax.psum(jnp.where(mine, value, jnp.zeros_like(value)), axis)  83.5 us
    psum x8, blocking collectives, shards(): lax.psum((jnp.sum(below * below), jnp.sum(jnp.where(row_ids == column + 1...  54.1 us
    psum x7, blocking collectives, shards(): inner = lax.psum(jnp.dot(current, refl, precision=exact), 'row')  40.1 us
  transfers between devices with their start and end apart: 1, of which 1 were waited for; matrix products, arithmetic and copies ran while one was open for 1% of the time, Pallas kernels for 0%

commit v1 on v0

--- a/solution.py
+++ b/solution.py
@@ -52,7 +52,7 @@
             (jnp.dot(vector, refl, precision=exact), jnp.dot(picker, vector, precision=exact)),
             "row",
         )
-        image = lax.psum(jnp.dot(matrix, piece, precision=exact), "col")
+        image = jnp.sum(lax.all_gather(jnp.dot(matrix, piece, precision=exact), "col"), axis=0)
         new_y = image - jnp.dot(wy_prod, coupling, precision=exact)
         new_t = -jnp.dot(factor, coupling, precision=exact)
         factor = factor.at[:, column].set(new_t).at[column, column].set(jnp.float32(1.0))

time: 907 us -> 886 us (0.977)
  blocking collectives: 444 us -> 422 us
    psum x8 -> x0, blocking collectives: 267 us -> none  [shards(): image = lax.psum(jnp.dot(matrix, piece, precision=exact), 'col')]
    all_gather x0 -> x8, blocking collectives: none -> 244 us  [shards(): lax.all_gather(jnp.dot(matrix, piece, precision=exact), 'col')]
where the time goes in v1:
time: 886 us; the launch traced here: 876 us
  blocking collectives  422 us (48%)
  matrix products  265 us (30%)
  waiting for transfers between devices  101 us (11%)
  between operations  31.4 us (4%)
  local copies, waits for them, and re-layouts  28.7 us (3%)
  other arithmetic  27.7 us (3%)
    dot_general x8, matrix products, shards(): jnp.dot(matrix, piece, precision=exact)  246 us
    all_gather x8, blocking collectives, shards(): lax.all_gather(jnp.dot(matrix, piece, precision=exact), 'col')  244 us
    psum x1, waiting for transfers between devices, spread(): return lax.psum(jnp.where(mine, value, jnp.zeros_like(value)), axis)  101 us
    psum x8, blocking collectives, spread(): return lax.psum(jnp.where(mine, value, jnp.zeros_like(value)), axis)  82.4 us
    psum x8, blocking collectives, shards(): lax.psum((jnp.sum(below * below), jnp.sum(jnp.where(row_ids == column + 1...  55.6 us
    psum x7, blocking collectives, shards(): inner = lax.psum(jnp.dot(current, refl, precision=exact), 'row')  39.5 us
    another operation x28, other arithmetic  18 us
  transfers between devices with their start and end apart: 1, of which 1 were waited for; matrix products, arithmetic and copies ran while one was open for 1% of the time, Pallas kernels for 0%

profile of v1, /device:TPU:0, one launch (start us, length us, event | category | flops | bytes accessed | tf_op | source)
XLA Modules:
  0.0 876.1 jit_solution(10953989410383108822)
XLA Ops:
  15.5 101.1 %all-reduce.22.cloned.1.call-done = f32[4096,8]{1,0:T(8,128)} async-done(((f32[4096,8]{1,0:T(8,128)}), f32[4096,8]{1,0:T(8,128)}) %all-reduce.22.cloned.1.call-update) | async-done | bytes 131088 | tf_op jit(solution)/shard_map/psum | solution.py:11
  116.7 15.4 %slice_reduce_fusion = (f32[4096]{0:T(1024)S(1)}, f32[4096]{0:T(1024)S(1)}, f32[4096]{0:T(1024)S(1)}, f32[4096]{0:T(1024)S(1)}, f32[4096]{0:T(1024)S(1)}, /*inde...) fusion(f32[4096,8]{1,0:T(8,128)} %all-reduce.22.cloned.1.call-done), kind=kLoop, calls=%fused_computation | loop fusion | bytes 262144 | tf_op jit(solution)/shard_map/slice | solution.py:28
  143.5 10.6 %all-reduce.18 = (f32[4096]{0:T(1024)S(1)}, f32[8]{0:T(128)S(1)}, f32[9]{0:T(128)S(1)}) all-reduce(f32[4096]{0:T(1024)S(1)} %broadcast_select_fusion.19, f32[8]{0:T(128)S(1)} %convolution_bitcast_fusion.36, f32[9]{0:T(128)S(1)} %convolution_bitcast_fusion.35), channel_id=1, replica_groups=mesh['row'=4,'col'=8] {'row'}, use_global_device_ids=true, to_apply=%region_6.7 | all-reduce | flops 4113 | bytes 32904 | tf_op jit(solution)/shard_map/psum | solution.py:11
  154.1 30.7 %fusion.122 = f32[1,4096]{1,0:T(1,128)S(1)} fusion(f32[2048,1]{0,1:T(1,128)S(1)} %bitcast.507, f32[4096,2048]{1,0:T(8,128)} %param.79), kind=kOutput, calls=%fused_computation.248 | convolution fusion | flops 100663296 | bytes 33579008 | tf_op jit(solution)/shard_map/dot_general | solution.py:55
  184.7 30.5 %all-gather = f32[32768]{0:T(1024)S(1)} all-gather(f32[4096]{0:T(1024)S(1)} %bitcast.450), channel_id=2, replica_groups=mesh['row'=4,'col'=8] {'col'}, dimensions={0}, use_global_device_ids=true | all-gather | bytes 147456 | tf_op jit(solution)/shard_map/all_gather | solution.py:55
  237.0 10.3 %all-reduce.16 = (f32[4096]{0:T(1024)S(1)}, f32[8]{0:T(128)S(1)}, f32[9]{0:T(128)S(1)}) all-reduce(f32[4096]{0:T(1024)S(1)} %broadcast_select_fusion.17, f32[8]{0:T(128)S(1)} %convolution_bitcast_fusion.33, f32[9]{0:T(128)S(1)} %convolution_bitcast_fusion.32), channel_id=1, replica_groups=mesh['row'=4,'col'=8] {'row'}, use_global_device_ids=true, to_apply=%region_16.17 | all-reduce | flops 4113 | bytes 32904 | tf_op jit(solution)/shard_map/psum | solution.py:11
  248.4 30.7 %fusion.123 = f32[1,4096]{1,0:T(1,128)S(1)} fusion(f32[2048,1]{0,1:T(1,128)S(1)} %bitcast.508, f32[4096,2048]{1,0:T(8,128)} %param.79), kind=kOutput, calls=%fused_computation.249 | convolution fusion | flops 100663296 | bytes 33579008 | tf_op jit(solution)/shard_map/dot_general | solution.py:55
  279.1 30.5 %all-gather.1 = f32[32768]{0:T(1024)S(1)} all-gather(f32[4096]{0:T(1024)S(1)} %bitcast.451), channel_id=3, replica_groups=mesh['row'=4,'col'=8] {'col'}, dimensions={0}, use_global_device_ids=true | all-gather | bytes 147456 | tf_op jit(solution)/shard_map/all_gather | solution.py:55
  329.9 10.3 %all-reduce.14 = (f32[4096]{0:T(1024)S(1)}, f32[8]{0:T(128)S(1)}, f32[9,1]{0,1:T(1,128)S(1)}) all-reduce(f32[4096]{0:T(1024)S(1)} %get-tuple-element.566, f32[8]{0:T(128)S(1)} %convolution_bitcast_fusion.30, f32[9,1]{0,1:T(1,128)S(1)} %convolution_bitcast_fusion.29), channel_id=1, replica_groups=mesh['row'=4,'col'=8] {'row'}, use_global_device_ids=true, to_apply=%region_26.27 | all-reduce | flops 4113 | bytes 32904 | tf_op jit(solution)/shard_map/psum | solution.py:11
  342.2 30.7 %fusion.125 = f32[1,4096]{1,0:T(1,128)S(1)} fusion(f32[2048,1]{0,1:T(1,128)S(1)} %bitcast.509, f32[4096,2048]{1,0:T(8,128)} %param.79), kind=kOutput, calls=%fused_computation.251 | convolution fusion | flops 100663296 | bytes 33579008 | tf_op jit(solution)/shard_map/dot_general | solution.py:55
  372.9 30.5 %all-gather.2 = f32[32768]{0:T(1024)S(1)} all-gather(f32[4096]{0:T(1024)S(1)} %bitcast.452), channel_id=4, replica_groups=mesh['row'=4,'col'=8] {'col'}, dimensions={0}, use_global_device_ids=true | all-gather | bytes 147456 | tf_op jit(solution)/shard_map/all_gather | solution.py:55
  423.2 10.3 %all-reduce.12 = (f32[4096]{0:T(1024)S(1)}, f32[8]{0:T(128)S(1)}, f32[9,1]{0,1:T(1,128)S(1)}) all-reduce(f32[4096]{0:T(1024)S(1)} %get-tuple-element.563, f32[8]{0:T(128)S(1)} %convolution_bitcast_fusion.27, f32[9,1]{0,1:T(1,128)S(1)} %convolution_bitcast_fusion.26), channel_id=1, replica_groups=mesh['row'=4,'col'=8] {'row'}, use_global_device_ids=true, to_apply=%region_36.37 | all-reduce | flops 4113 | bytes 32904 | tf_op jit(solution)/shard_map/psum | solution.py:11
  435.1 30.7 %fusion.127 = f32[1,4096]{1,0:T(1,128)S(1)} fusion(f32[2048,1]{0,1:T(1,128)S(1)} %bitcast.510, f32[4096,2048]{1,0:T(8,128)} %param.79), kind=kOutput, calls=%fused_computation.253 | convolution fusion | flops 100663296 | bytes 33579008 | tf_op jit(solution)/shard_map/dot_general | solution.py:55
  465.8 30.7 %all-gather.3 = f32[32768]{0:T(1024)S(1)} all-gather(f32[4096]{0:T(1024)S(1)} %bitcast.453), channel_id=5, replica_groups=mesh['row'=4,'col'=8] {'col'}, dimensions={0}, use_global_device_ids=true | all-gather | bytes 147456 | tf_op jit(solution)/shard_map/all_gather | solution.py:55
  516.3 10.3 %all-reduce.10 = (f32[4096]{0:T(1024)S(1)}, f32[8]{0:T(128)S(1)}, f32[9,1]{0,1:T(1,128)S(1)}) all-reduce(f32[4096]{0:T(1024)S(1)} %get-tuple-element.560, f32[8]{0:T(128)S(1)} %convolution_bitcast_fusion.24, f32[9,1]{0,1:T(1,128)S(1)} %convolution_bitcast_fusion.23), channel_id=1, replica_groups=mesh['row'=4,'col'=8] {'row'}, use_global_device_ids=true, to_apply=%region_46.47 | all-reduce | flops 4113 | bytes 32904 | tf_op jit(solution)/shard_map/psum | solution.py:11
  528.3 30.7 %fusion.129 = f32[1,4096]{1,0:T(1,128)S(1)} fusion(f32[2048,1]{0,1:T(1,128)S(1)} %bitcast.511, f32[4096,2048]{1,0:T(8,128)} %param.79), kind=kOutput, calls=%fused_computation.255 | convolution fusion | flops 100663296 | bytes 33579008 | tf_op jit(solution)/shard_map/dot_general | solution.py:55
  559.0 30.6 %all-gather.4 = f32[32768]{0:T(1024)S(1)} all-gather(f32[4096]{0:T(1024)S(1)} %bitcast.454), channel_id=6, replica_groups=mesh['row'=4,'col'=8] {'col'}, dimensions={0}, use_global_device_ids=true | all-gather | bytes 147456 | tf_op jit(solution)/shard_map/all_gather | solution.py:55
  621.4 30.7 %fusion.131 = f32[1,4096]{1,0:T(1,128)S(1)} fusion(f32[2048,1]{0,1:T(1,128)S(1)} %bitcast.512, f32[4096,2048]{1,0:T(8,128)} %param.79), kind=kOutput, calls=%fused_computation.257 | convolution fusion | flops 100663296 | bytes 33579008 | tf_op jit(solution)/shard_map/dot_general | solution.py:55
  652.1 30.5 %all-gather.5 = f32[32768]{0:T(1024)S(1)} all-gather(f32[4096]{0:T(1024)S(1)} %bitcast.455), channel_id=7, replica_groups=mesh['row'=4,'col'=8] {'col'}, dimensions={0}, use_global_device_ids=true | all-gather | bytes 147456 | tf_op jit(solution)/shard_map/all_gather | solution.py:55
  714.5 30.7 %fusion.133 = f32[1,4096]{1,0:T(1,128)S(1)} fusion(f32[2048,1]{0,1:T(1,128)S(1)} %bitcast.513, f32[4096,2048]{1,0:T(8,128)} %param.79), kind=kOutput, calls=%fused_computation.259 | convolution fusion | flops 100663296 | bytes 33579008 | tf_op jit(solution)/shard_map/dot_general | solution.py:55
  745.2 30.5 %all-gather.6 = f32[32768]{0:T(1024)S(1)} all-gather(f32[4096]{0:T(1024)S(1)} %bitcast.456), channel_id=8, replica_groups=mesh['row'=4,'col'=8] {'col'}, dimensions={0}, use_global_device_ids=true | all-gather | bytes 147456 | tf_op jit(solution)/shard_map/all_gather | solution.py:55
  794.4 10.3 %all-reduce.4 = (f32[4096]{0:T(1024)S(1)}, f32[8]{0:T(128)S(1)}) all-reduce(f32[4096]{0:T(1024)S(1)} %get-tuple-element.551, f32[8]{0:T(128)S(1)} %convolution_bitcast_fusion.15), channel_id=1, replica_groups=mesh['row'=4,'col'=8] {'row'}, use_global_device_ids=true, to_apply=%region_75.76 | all-reduce | flops 4104 | bytes 32832 | tf_op jit(solution)/shard_map/psum | solution.py:11
  806.5 30.7 %fusion.135 = f32[1,4096]{1,0:T(1,128)S(1)} fusion(f32[2048,1]{0,1:T(1,128)S(1)} %bitcast.506, f32[4096,2048]{1,0:T(8,128)} %param.79), kind=kOutput, calls=%fused_computation.261 | convolution fusion | flops 100663296 | bytes 33579008 | tf_op jit(solution)/shard_map/dot_general | solution.py:55
  837.2 30.6 %all-gather.7 = f32[32768]{0:T(1024)S(1)} all-gather(f32[4096]{0:T(1024)S(1)} %bitcast.457), channel_id=9, replica_groups=mesh['row'=4,'col'=8] {'col'}, dimensions={0}, use_global_device_ids=true | all-gather | bytes 147456 | tf_op jit(solution)/shard_map/all_gather | solution.py:55
  (216 shorter events, 176.2 us)
Async XLA Ops:
  7.2 109.5 %all-reduce.22.cloned.1.call-start = ((), (), s32[]{:S(2)}) async-start(), calls=%async_computation | async-start | bytes 4194304 | tf_op jit(solution)/shard_map/psum | solution.py:11
  805.4 63.7 %copy-start = (f32[4096,8]{0,1:T(8,128)}, f32[4096,8]{0,1:T(8,128)S(1)}, u32[]{:S(2)}) copy-start(f32[4096,8]{0,1:T(8,128)S(1)} %scatter.189) | copy-start | bytes 393220
  868.2 0.9 copy-start.1
Sparse Core Ops, SparseCore 0:
  11.6 105.0 all-reduce.21
